TPU v7x, 128 devices: a whole 4x4x4 slice. The times are simulated.
128 devices in a mesh: left: 16 (over y, x), right: 8 (over z, core).
Axes of the slice: x: 4, y: 4, z: 4, core: 2. Of those that a mesh axis runs over, the one named last changes fastest.
Arguments:
- signal: float32 [512, 512, 2048], P(None, 'left', 'right'), may hold values from -6 to 6
- symbol_x: float32 [512], replicated, may hold values from 0.3 to 3
- symbol_y: float32 [512], replicated, may hold values from 0.3 to 3
- symbol_z: float32 [2048], replicated, may hold values from 0.3 to 3
Outputs:
- spectrum: float32 [256, 256, 1024], P('left', 'right')
All inputs are finite; a program needn't handle non-finite values.
Results may differ from a plain program's by a relative error of at most 0.000096.
Values sent between devices are 32-bit elements; how exact they have to be, the bound alone decides.
A program may use at most 128 MiB of HBM per device.

v0:
```python
import jax
import jax.numpy as jnp
from jax import lax
from jax.sharding import PartitionSpec as P


def transform_table(count):
    rank = jnp.arange(count)
    angle = (
        jnp.pi
        / (4 * count)
        * ((2 * rank[:, None] + 1) * (2 * rank[None, :] + 1) % (8 * count)).astype(jnp.float32)
    )
    return jnp.cos(angle) * (2.0 / count) ** 0.5


def transform_dim(values, dim):
    moved = jnp.tensordot(
        values,
        transform_table(values.shape[dim]),
        axes=([dim], [0]),
        precision=lax.Precision.HIGHEST,
    )
    return jnp.moveaxis(moved, -1, dim)


def body(signal, symbol_x, symbol_y, symbol_z):
    part_values = signal
    part_values = transform_dim(part_values, 0)
    part_values = lax.slice_in_dim(part_values, 0, part_values.shape[0] // 2, axis=0)
    part_values = lax.all_to_all(part_values, "left", split_axis=0, concat_axis=1, tiled=True)
    part_values = transform_dim(part_values, 1)
    pencil_values = lax.slice_in_dim(part_values, 0, part_values.shape[1] // 2, axis=1)
    pencil_values = lax.all_to_all(pencil_values, "right", split_axis=1, concat_axis=2, tiled=True)
    pencil_values = transform_dim(pencil_values, 2)
    pencil_values = lax.slice_in_dim(pencil_values, 0, pencil_values.shape[2] // 2, axis=2)
    share_x = pencil_values.shape[0]
    part_x = lax.dynamic_slice_in_dim(symbol_x, lax.axis_index("left") * share_x, share_x)
    share_y = pencil_values.shape[1]
    part_y = lax.dynamic_slice_in_dim(symbol_y, lax.axis_index("right") * share_y, share_y)
    symbol = (
        part_x[:, None, None]
        + part_y[None, :, None]
        + symbol_z[: pencil_values.shape[2]][None, None, :]
    )
    pencil_values = pencil_values * ((1.0 - 0.2 * symbol) / (1.0 + 0.2 * symbol))
    return pencil_values


def solution(mesh):
    in_specs = (P(None, "left", "right"), P(), P(), P())
    out_specs = P("left", "right", None)
    return jax.shard_map(body, mesh=mesh, in_specs=in_specs, out_specs=out_specs, check_vma=False)
```

profile of v0, /device:TPU:1, one launch (start us, length us, event | category | flops | bytes accessed | tf_op | source)
XLA Modules:
  0.0 268.1 jit_solution(16005972733140599428)
XLA Ops:
  0.0 3.9 %fusion.16 = f32[512,512,1]{1,0,2:T(8,128)S(1)} fusion(s32[512]{0:T(512)S(1)} %multiply_add_fusion.1), kind=kLoop, calls=%fused_computation.26 | loop fusion | flops 3932160 | bytes 1050624 | tf_op jit(solution)/shard_map/mul | solution.py:14
  3.9 24.2 %fusion.6 = f32[256,32,256]{2,0,1:T(8,128)S(1)} fusion(f32[512,32,256]{2,1,0:T(8,128)} %param.4, f32[512,512,1]{1,0,2:T(8,128)S(1)} %fusion.16), kind=kOutput, calls=%fused_computation.11 | convolution fusion | flops 12884901888 | bytes 25690112 | tf_op jit(solution)/shard_map/dot_general | solution.py:18
  28.1 4.9 %copy.24 = f32[256,32,256]{2,1,0:T(8,128)S(1)} copy(f32[256,32,256]{2,0,1:T(8,128)S(1)} %fusion.6) | data formatting | bytes 16777216 | tf_op jit(solution)/shard_map/slice | solution.py:30
  32.9 102.1 %all_to_all.36 = f32[256,32,256]{2,1,0:T(8,128)} all-to-all(f32[256,32,256]{2,1,0:T(8,128)S(1)} %copy.24), channel_id=1, replica_groups=mesh['left'=16,'right'=8] {'left'}, dimensions={0} | all-to-all | bytes 16777216 | tf_op jit(solution)/shard_map/all_to_all | solution.py:31
  135.1 4.3 %copy.25 = f32[16,16,32,256]{3,2,1,0:T(8,128)S(1)} copy(f32[16,16,32,256]{3,2,0,1:T(8,128)} %bitcast.20) | data formatting | bytes 16777216 | tf_op jit(solution)/shard_map/all_to_all | solution.py:31
  139.3 18.7 %convolution_bitcast_fusion = f32[16,512,256]{1,2,0:T(8,128)S(1)} fusion(f32[16,512,256]{2,1,0:T(8,128)S(1)} %bitcast.19, s32[512]{0:T(512)S(1)} %multiply_add_fusion.1), kind=kOutput, calls=%fused_computation.15 | convolution fusion | flops 12888834048 | bytes 16779264 | tf_op jit(solution)/shard_map/dot_general | solution.py:18
  158.0 2.5 slice.19
  160.6 5.5 %copy.27 = f32[16,256,256]{2,0,1:T(8,128)} copy(f32[16,256,256]{1,2,0:T(8,128)} %slice.19) | data formatting | bytes 8388608 | tf_op jit(solution)/shard_map/slice | solution.py:33
  166.0 7.6 %all-to-all-start.1 = ((f32[16,256,256]{2,0,1:T(8,128)}), f32[16,256,256]{2,0,1:T(8,128)}, u32[]{:S(2)}, u32[]{:S(2)}) async-start(f32[16,256,256]{2,0,1:T(8,128)} %copy.27), calls=%async_computation.1 | async-start | bytes 8388608 | tf_op jit(solution)/shard_map/all_to_all | solution.py:34
  173.7 0.8 dynamic_slice.7
  174.4 0.8 dynamic_slice.6
  175.2 0.1 broadcast_add_fusion
  175.3 63.1 %fusion.4 = f32[2048,2048,1]{1,0,2:T(8,128)} fusion(s32[2048]{0:T(1024)S(1)} %multiply_add_fusion), kind=kLoop, calls=%fused_computation.9 | loop fusion | flops 62914560 | bytes 16785408 | tf_op jit(solution)/shard_map/mul | solution.py:14
  238.4 0.0 all-to-all-done.1
  238.4 0.0 slice-start
  238.4 6.6 %copy.29 = f32[16,32,8,256]{3,2,1,0:T(8,128)} copy(f32[16,32,8,256]{3,0,1,2:T(8,128)} %bitcast.8) | data formatting | bytes 8388608 | tf_op jit(solution)/shard_map/all_to_all | solution.py:34
  245.0 4.9 %all_to_all.33 = f32[16,32,2048]{2,1,0:T(8,128)} reshape(f32[16,32,8,256]{3,2,1,0:T(8,128)} %copy.29) | data formatting | bytes 8388608 | tf_op jit(solution)/shard_map/all_to_all | solution.py:34
  249.8 0.0 slice-done
  249.8 18.1 %divide_multiply_fusion = f32[16,32,1024]{2,1,0:T(8,128)} fusion(f32[16,32,2048]{2,1,0:T(8,128)} %all_to_all.33, f32[2048,2048,1]{1,0,2:T(8,128)} %fusion.4, f32[1024]{0:T(1024)S(1)} %slice-done, f32[16,32]{1,0:T(8,128)S(1)} %broadcast_add_fusion), kind=kOutput, calls=%fused_computation.16 | convolution fusion | flops 12888047616 | bytes 14686208 | tf_op jit(solution)/shard_map/dot_general | solution.py:18
  (2 shorter events, 0.0 us)
Async XLA Ops:
  166.0 72.3 %all-to-all-start.1 = ((f32[16,256,256]{2,0,1:T(8,128)}), f32[16,256,256]{2,0,1:T(8,128)}, u32[]{:S(2)}, u32[]{:S(2)}) async-start(f32[16,256,256]{2,0,1:T(8,128)} %copy.27), calls=%async_computation.1 | async-start | bytes 8388608 | tf_op jit(solution)/shard_map/all_to_all | solution.py:34
  238.4 11.5 %slice-start = ((f32[2048]{0:T(1024)}), f32[1024]{0:T(1024)S(1)}, s32[]{:S(2)}) async-start(f32[2048]{0:T(1024)} %param.7), calls=%async_computation.2 | async-start | bytes 8192 | tf_op jit(solution)/shard_map/slice | solution.py:44
where the time goes:
time: 272 us; the launch traced here: 268 us
  blocking collectives  102 us (38%)
  other arithmetic  67.1 us (25%)
  matrix products  61 us (22%)
  local copies, waits for them, and re-layouts  30.1 us (11%)
  starting transfers between devices  7.63 us (3%)
    all_to_all x1, blocking collectives, body(): lax.all_to_all(part_values, 'left', split_axis=0, concat_axis=1, tiled=True)  102 us
    mul x2, other arithmetic, transform_table(): return jnp.cos(angle) * (2.0 / count) ** 0.5  67 us
    dot_general x3, matrix products, transform_dim(): jnp.tensordot(values, transform_table(values.shape[dim]), axes=([dim], [0...  61 us
    all_to_all x2, local copies, waits for them, and re-layouts, body(): lax.all_to_all(pencil_values, 'right', split_axis=1, concat_axis=2, tiled...  11.5 us
    slice x2, local copies, waits for them, and re-layouts, body(): lax.slice_in_dim(part_values, 0, part_values.shape[1] // 2, axis=1)  7.99 us
    all_to_all x1, starting transfers between devices, body(): lax.all_to_all(pencil_values, 'right', split_axis=1, concat_axis=2, tiled...  7.63 us
  transfers between devices with their start and end apart: 1, of which 0 were waited for; matrix products, arithmetic and copies ran while one was open for 24% of the time, Pallas kernels for 0%

commit v1 on v0

v1 whole, which is shorter than its diff:
```python
import functools

import jax
import jax.numpy as jnp
import numpy as np
from jax import lax
from jax.experimental import pallas as pl
from jax.experimental.pallas import tpu as pltpu
from jax.sharding import PartitionSpec as P

MESH = pl.DeviceIdType.MESH
F32 = jnp.float32
BF16 = jnp.bfloat16
NX, NY, NZ = 512, 512, 2048
KX, KY, KZ = NX // 2, NY // 2, NZ // 2
LEFT, RIGHT = 16, 8
YL, ZL = NY // LEFT, NZ // RIGHT
XO, YO = KX // LEFT, KY // RIGHT
PITCH = 72
EARLY = 4
FINE = 64


def half_table(count):
    i = np.arange(count, dtype=np.int64)[:, None]
    k = np.arange(count // 2, dtype=np.int64)[None, :]
    phase = (2 * i + 1) * (2 * k + 1) % (8 * count)
    return np.cos(np.pi / (4 * count) * phase) * np.sqrt(2.0 / count)


def split_table(count):
    table = np.ascontiguousarray(half_table(count).T).astype(np.float32)
    high = table.astype(BF16)
    low = (table - high.astype(np.float32)).astype(BF16)
    return np.concatenate([high, high, low], axis=1)


def factor_tables(count):
    k = 2 * np.arange(count // 2, dtype=np.int64)[None, :] + 1
    a = np.arange(count // FINE, dtype=np.int64)[:, None]
    b = np.arange(FINE, dtype=np.int64)[:, None]
    coarse = np.pi / (4 * count) * (2 * FINE * a * k % (8 * count))
    fine = np.pi / (4 * count) * ((2 * b + 1) * k % (8 * count))
    scale = np.sqrt(2.0 / count)
    return (
        np.stack([np.cos(coarse) * scale, np.sin(coarse) * scale]).astype(np.float32),
        np.stack([np.cos(fine), np.sin(fine)]).astype(np.float32),
    )


def parts(values):
    high = values.astype(BF16)
    low = (values - high.astype(F32)).astype(BF16)
    return high, low


def dot(a, b):
    return jnp.dot(a, b, preferred_element_type=F32)


def kernel(
    s_ref, h_ref, coarse_ref, fine_ref, sx_ref, sy_ref, sz_ref, o_ref,
    slabs, table, coarse, fine, ztable, t1, r1, t2, q, zlhs, sym, result,
    slab_sem, table_sem, lsend, lrecv, qsend, qrecv, out_sem,
):
    left = lax.axis_index("left")
    right = lax.axis_index("right")
    cy, cx = left // 4, left % 4

    def left_peer(p, sign):
        return ((cy + sign * (p // 4) + 4) % 4) * 4 + (cx + sign * (p % 4) + 4) % 4

    def right_peer(p, sign):
        return ((right // 2 + sign * (p // 2) + 4) % 4) * 2 + (right + p) % 2

    barrier = pltpu.get_barrier_semaphore()
    for p in range(1, LEFT):
        pl.semaphore_signal(barrier, inc=1, device_id=(left_peer(p, -1), right), device_id_type=MESH)
    for p in range(1, RIGHT):
        pl.semaphore_signal(barrier, inc=1, device_id=(left, right_peer(p, -1)), device_id_type=MESH)

    def slab_copy(i):
        return pltpu.make_async_copy(
            s_ref.at[:, pl.ds(pl.multiple_of(i // 2 * 8, 8), 8), pl.ds(pl.multiple_of(i % 2 * 128, 128), 128)],
            slabs.at[i],
            slab_sem.at[i],
        )

    table_copies = [
        pltpu.make_async_copy(h_ref, table, table_sem.at[0]),
        pltpu.make_async_copy(coarse_ref, coarse, table_sem.at[1]),
        pltpu.make_async_copy(fine_ref, fine, table_sem.at[2]),
    ]
    table_copies[0].start()
    for i in range(8):
        slab_copy(i).start()
    table_copies[1].start()
    table_copies[2].start()
    table_copies[0].wait()

    def x_slab(i):
        slab_copy(i).wait()
        rows = slabs.at[i].reshape(NX * 8, 128)
        for pair in range(4):
            data = jnp.concatenate(
                [rows[pl.ds(2 * pair + e, NX, stride=8), :] for e in range(2)], axis=1
            )
            high, low = parts(data)
            modes = dot(table[...], jnp.concatenate([high, low, high], axis=0))
            for e in range(2):
                t1[pl.ds(i * 8 + 2 * pair + e, KX, stride=PITCH), :] = modes[:, 128 * e : 128 * (e + 1)]

    def left_copy(x, p, first, count):
        peer = left_peer(p, 1)
        return pltpu.make_async_remote_copy(
            src_ref=t1.at[pl.ds(pl.multiple_of((peer * XO + x) * PITCH + first, 8), count), :],
            dst_ref=r1.at[pl.ds(pl.multiple_of((x * LEFT + left) * 64 + first, 8), count), :],
            send_sem=lsend.at[x],
            recv_sem=lrecv.at[x],
            device_id=(peer, right),
            device_id_type=MESH,
        )

    def x_step(b, carry):
        x_slab(2 * b)
        x_slab(2 * b + 1)

        @pl.when(b == 0)
        def _():
            pl.semaphore_wait(barrier, LEFT + RIGHT - 2)

        def send(j, carry):
            left_copy(j // (LEFT - 1), j % (LEFT - 1) + 1, b * 16, 16).start()
            return carry

        lax.fori_loop(0, EARLY * (LEFT - 1), send, 0)
        return carry

    lax.fori_loop(0, 4, x_step, 0)

    def send(j, carry):
        left_copy(EARLY + j // (LEFT - 1), j % (LEFT - 1) + 1, 0, 64).start()
        return carry

    lax.fori_loop(0, (XO - EARLY) * (LEFT - 1), send, 0)

    def own(x, carry):
        r1[pl.ds(pl.multiple_of((x * LEFT + left) * 64, 8), 64), :] = t1[
            pl.ds(pl.multiple_of((left * XO + x) * PITCH, 8), 64), :
        ]
        return carry

    lax.fori_loop(0, XO, own, 0)

    table_copies[1].wait()
    table_copies[2].wait()

    def z_rows(a, carry):
        cos_a, sin_a = coarse[0, pl.ds(a, 1), :], coarse[1, pl.ds(a, 1), :]
        block = cos_a * fine[0] - sin_a * fine[1]
        high, low = parts(block)
        for n in range(4):
            ztable[n, pl.ds(pl.multiple_of(a * FINE, FINE), FINE), :] = high[:, 256 * n : 256 * (n + 1)]
            ztable[n, pl.ds(pl.multiple_of(NZ + a * FINE, FINE), FINE), :] = low[:, 256 * n : 256 * (n + 1)]
        return carry

    lax.fori_loop(0, NZ // FINE, z_rows, 0)

    row = lax.broadcasted_iota(jnp.int32, (YO, 128), 0)
    of_y = jnp.zeros((YO, 128), F32)
    for j in range(YO):
        of_y = jnp.where(row == j, sy_ref[right * YO + j], of_y)
    sym[...] = of_y

    def right_copy(x, p):
        peer = right_peer(p, 1)
        return pltpu.make_async_remote_copy(
            src_ref=t2.at[x, pl.ds(pl.multiple_of(peer * YO, YO), YO), :],
            dst_ref=q.at[x, right],
            send_sem=qsend.at[x],
            recv_sem=qrecv.at[x],
            device_id=(left, peer),
            device_id_type=MESH,
        )

    def out_copy(x):
        return pltpu.make_async_copy(result.at[x], o_ref.at[x], out_sem.at[x])

    def left_bytes(x):
        return r1.at[pl.ds(pl.multiple_of(x * 1024, 1024), 64 * (LEFT - 1)), :]

    def right_bytes(x):
        return q.at[x, pl.ds(0, RIGHT - 1)]

    def y_step(x):
        pltpu.make_async_copy(left_bytes(x), left_bytes(x), lrecv.at[x]).wait()
        lines = r1[pl.ds(pl.multiple_of(x * 1024, 1024), 1024), :].reshape(64, 2, 8, 128)
        data = jnp.concatenate([lines[:, e].reshape(NY, 128) for e in range(2)], axis=1)
        high, low = parts(data)
        t2[x] = dot(table[...], jnp.concatenate([high, low, high], axis=0))
        for p in range(1, RIGHT):
            right_copy(x, p).start()
        q[x, right] = t2[x, pl.ds(pl.multiple_of(right * YO, YO), YO), :]

    def z_step(x):
        pltpu.make_async_copy(right_bytes(x), right_bytes(x), qrecv.at[x]).wait()
        for k in range(RIGHT):
            high, low = parts(q[x, k])
            zlhs[0:YO, 256 * k : 256 * (k + 1)] = high
            zlhs[YO : 2 * YO, 256 * k : 256 * (k + 1)] = low
        of_xy = sx_ref[left * XO + x] + sym[...]
        of_xy = jnp.concatenate([of_xy, of_xy], axis=1)
        for n in range(4):
            both = dot(zlhs[...], ztable[n, 0:NZ, :])
            rest = dot(zlhs[0:YO, :], ztable[n, NZ : 2 * NZ, :])
            symbol = of_xy + sz_ref[:, 256 * n : 256 * (n + 1)]
            ratio = (1.0 - 0.2 * symbol) / (1.0 + 0.2 * symbol)
            result[x, :, 256 * n : 256 * (n + 1)] = (both[0:YO] + (both[YO:] + rest)) * ratio
        out_copy(x).start()

    def step(i, carry):
        @pl.when(i < XO)
        def _():
            y_step(i)

        @pl.when(i > 0)
        def _():
            z_step(i - 1)

        return carry

    lax.fori_loop(0, XO + 1, step, 0)

    def finish(x, carry):
        pltpu.make_async_copy(left_bytes(x), left_bytes(x), lsend.at[x]).wait()
        pltpu.make_async_copy(right_bytes(x), right_bytes(x), qsend.at[x]).wait()
        out_copy(x).wait()
        return carry

    lax.fori_loop(0, XO, finish, 0)


def body(signal, symbol_x, symbol_y, symbol_z):
    coarse, fine = factor_tables(NZ)
    table = split_table(NX)
    dma = pltpu.SemaphoreType.DMA
    any_space = pl.BlockSpec(memory_space=pl.ANY)
    smem = pl.BlockSpec(memory_space=pltpu.SMEM)
    return pl.pallas_call(
        kernel,
        out_shape=jax.ShapeDtypeStruct((XO, YO, KZ), F32),
        in_specs=[any_space, any_space, any_space, any_space, smem, smem, pl.BlockSpec(memory_space=pltpu.VMEM)],
        out_specs=any_space,
        scratch_shapes=[
            pltpu.VMEM((8, NX, 8, 128), F32),
            pltpu.VMEM(table.shape, BF16),
            pltpu.VMEM(coarse.shape, F32),
            pltpu.VMEM(fine.shape, F32),
            pltpu.VMEM((4, 2 * NZ, 256), BF16),
            pltpu.VMEM((KX * PITCH, 128), F32),
            pltpu.VMEM((XO * LEFT * 64, 128), F32),
            pltpu.VMEM((XO, KY, ZL), F32),
            pltpu.VMEM((XO, RIGHT, YO, ZL), F32),
            pltpu.VMEM((2 * YO, NZ), BF16),
            pltpu.VMEM((YO, 128), F32),
            pltpu.VMEM((XO, YO, KZ), F32),
            dma((8,)),
            dma((3,)),
            dma((XO,)),
            dma((XO,)),
            dma((XO,)),
            dma((XO,)),
            dma((XO,)),
        ],
        compiler_params=pltpu.CompilerParams(
            collective_id=0, has_side_effects=True, vmem_limit_bytes=67043328
        ),
    )(
        signal,
        jnp.asarray(table),
        jnp.asarray(coarse),
        jnp.asarray(fine),
        symbol_x,
        symbol_y,
        symbol_z.reshape(1, NZ),
    )


def solution(mesh):
    in_specs = (P(None, "left", "right"), P(), P(), P())
    out_specs = P("left", "right", None)
    return jax.shard_map(body, mesh=mesh, in_specs=in_specs, out_specs=out_specs, check_vma=False)
```

time: 272 us -> 118 us (0.43); the launches traced: 268 us -> 118 us
  Pallas kernels: 0 us -> 114 us
  blocking collectives: 102 us -> 0 us
  other arithmetic: 67.1 us -> 0 us
  matrix products: 61 us -> 0 us
  local copies, waits for them, and re-layouts: 30.1 us -> 3.16 us
  starting transfers between devices: 7.63 us -> 0 us
    pallas_call x0 -> x1, Pallas kernels: none -> 114 us  [body(): pl.pallas_call(kernel, out_shape=jax.ShapeDtypeStruct((XO, YO, KZ), F32),...]
    all_to_all x1 -> x0, blocking collectives: 102 us -> none  [body(): lax.all_to_all(part_values, 'left', split_axis=0, concat_axis=1, tiled=True)]
    mul x2 -> x0, other arithmetic: 67 us -> none  [transform_table(): return jnp.cos(angle) * (2.0 / count) ** 0.5]
    dot_general x3 -> x0, matrix products: 61 us -> none  [transform_dim(): jnp.tensordot(values, transform_table(values.shape[dim]), axes=([dim], [0...]
    all_to_all x3 -> x0, local copies, waits for them, and re-layouts: 15.7 us -> none  [the longest x2 11.5 us: body(): lax.all_to_all(pencil_values, 'right', split_axis=1, concat_axis=2, tiled...]
    slice x5 -> x0, local copies, waits for them, and re-layouts: 12.8 us -> none  [the longest x2 7.99 us: body(): lax.slice_in_dim(part_values, 0, part_values.shape[1] // 2, axis=1)]
    all_to_all x1 -> x0, starting transfers between devices: 7.63 us -> none  [body(): lax.all_to_all(pencil_values, 'right', split_axis=1, concat_axis=2, tiled...]
    unnamed x0 -> x1, local copies, waits for them, and re-layouts: none -> 3.16 us
  transfers between devices with their start and end apart: 1 -> 0, of which waited for: 0 -> 0; matrix products, arithmetic and copies ran while one was open for 24% -> 0% of each run, Pallas kernels for 0% -> 0%
where the time goes in v1:
time: 118 us
  Pallas kernels  114 us (97%)
  local copies, waits for them, and re-layouts  3.16 us (3%)
    pallas_call x1, Pallas kernels, body(): pl.pallas_call(kernel, out_shape=jax.ShapeDtypeStruct((XO, YO, KZ), F32),...  114 us
    unnamed x1, local copies, waits for them, and re-layouts  3.16 us

profile of v1, /device:TPU:1, one launch (start us, length us, event | category | flops | bytes accessed | tf_op | source)
XLA Modules:
  0.0 117.6 jit_solution(15038583558666842435)
XLA Ops:
  0.0 114.5 %shard_map.73 = f32[16,32,1024]{2,1,0:T(8,128)} custom-call(f32[512,32,256]{2,1,0:T(8,128)} %s_ref.1, bf16[256,1536]{1,0:T(8,128)(2,1)} %constant.6.clone.h_ref, f32[2,32,1024]{2,1,0:T(8,128)} %constant.7.clone.coarse_ref, f32[2,64,1024]{2,1,0:T(8,128)} %constant.8.clone.fine_ref, f32[512]{0:T(512)} %sx_ref.1, f32[512]{0:T(512)} %sy_ref.1, f32[1,2048]{1,0:T(1,128)} %bitcast.1), custom_call_target="tpu_custom_call" | custom-call | tf_op jit(solution)/shard_map/pallas_call | solution.py:249
  114.5 3.2 %copy.9 = f32[16,32,1024]{2,1,0:T(8,128)} copy(f32[16,32,1024]{2,1,0:T(8,128)} %shard_map.73) | data formatting | bytes 4194304

commit v2 on v1

v2 whole, which is shorter than its diff:
```python
import functools

import jax
import jax.numpy as jnp
import numpy as np
from jax import lax
from jax.experimental import pallas as pl
from jax.experimental.pallas import tpu as pltpu
from jax.sharding import PartitionSpec as P

MESH = pl.DeviceIdType.MESH
F32 = jnp.float32
BF16 = jnp.bfloat16
NX, NY, NZ = 512, 512, 2048
KX, KY, KZ = NX // 2, NY // 2, NZ // 2
LEFT, RIGHT = 16, 8
YL, ZL = NY // LEFT, NZ // RIGHT
XO, YO = KX // LEFT, KY // RIGHT
PITCH = 72
XA = XO - RIGHT
EARLY = 2
FINE = 64


def half_table(count):
    i = np.arange(count, dtype=np.int64)[:, None]
    k = np.arange(count // 2, dtype=np.int64)[None, :]
    phase = (2 * i + 1) * (2 * k + 1) % (8 * count)
    return np.cos(np.pi / (4 * count) * phase) * np.sqrt(2.0 / count)


def split_table(count, order):
    table = np.ascontiguousarray(half_table(count).T[order]).astype(np.float32)
    high = table.astype(BF16)
    low = (table - high.astype(np.float32)).astype(BF16)
    return np.concatenate([high, high, low], axis=1)


def x_order():
    block = np.arange(LEFT) * XO
    second = block[None, :] + XA + np.arange(RIGHT)[:, None]
    first = block[:, None] + np.arange(XA)[None, :]
    return np.concatenate([second.reshape(-1), first.reshape(-1)])


def factor_tables(count):
    k = 2 * np.arange(count // 2, dtype=np.int64)[None, :] + 1
    a = np.arange(count // FINE, dtype=np.int64)[:, None]
    b = np.arange(FINE, dtype=np.int64)[:, None]
    coarse = np.pi / (4 * count) * (2 * FINE * a * k % (8 * count))
    fine = np.pi / (4 * count) * ((2 * b + 1) * k % (8 * count))
    scale = np.sqrt(2.0 / count)
    return (
        np.stack([np.cos(coarse) * scale, np.sin(coarse) * scale]).astype(np.float32),
        np.stack([np.cos(fine), np.sin(fine)]).astype(np.float32),
    )


def parts(values):
    high = values.astype(BF16)
    low = (values - high.astype(F32)).astype(BF16)
    return high, low


def dot(a, b):
    return jnp.dot(a, b, preferred_element_type=F32)


def kernel(
    s_ref, hx_ref, hy_ref, coarse_ref, fine_ref, sx_ref, sy_ref, sz_ref, o_ref,
    slabs, xtable, ytable, coarse, fine, ztable, t1, r1, t2, q, w, v, u, t3, zlhs, sym, result,
    slab_sem, table_sem, lsend, lrecv, qsend, qrecv, wsend, wrecv, usend, urecv, bsend, brecv, out_sem,
):
    left = lax.axis_index("left")
    right = lax.axis_index("right")
    cy, cx = left // 4, left % 4

    def left_peer(p, sign):
        return ((cy + sign * (p // 4) + 4) % 4) * 4 + (cx + sign * (p % 4) + 4) % 4

    def right_peer(p, sign):
        return ((right // 2 + sign * (p // 2) + 4) % 4) * 2 + (right + p) % 2

    barrier = pltpu.get_barrier_semaphore()
    for p in range(1, LEFT):
        pl.semaphore_signal(barrier, inc=1, device_id=(left_peer(p, -1), right), device_id_type=MESH)
    for p in range(1, RIGHT):
        pl.semaphore_signal(barrier, inc=1, device_id=(left, right_peer(p, -1)), device_id_type=MESH)

    def slab_copy(i):
        return pltpu.make_async_copy(
            s_ref.at[:, pl.ds(pl.multiple_of(i // 2 * 8, 8), 8), pl.ds(pl.multiple_of(i % 2 * 128, 128), 128)],
            slabs.at[i],
            slab_sem.at[i],
        )

    table_copies = [
        pltpu.make_async_copy(hx_ref, xtable, table_sem.at[0]),
        pltpu.make_async_copy(coarse_ref, coarse, table_sem.at[1]),
        pltpu.make_async_copy(fine_ref, fine, table_sem.at[2]),
        pltpu.make_async_copy(hy_ref, ytable, table_sem.at[3]),
    ]
    slab_copy(0).start()
    table_copies[0].start()
    slab_copy(1).start()
    table_copies[0].wait()

    sym[...] = jnp.broadcast_to(sy_ref[:, 0:KY], (128, KY)).T

    def x_slab(i):
        rows = slabs.at[i].reshape(NX * 8, 128)
        lines = t1.reshape(KX * PITCH, 128)
        for pair in range(4):
            data = jnp.concatenate(
                [rows[pl.ds(2 * pair + e, NX, stride=8), :] for e in range(2)], axis=1
            )
            high, low = parts(data)
            modes = dot(xtable[...], jnp.concatenate([high, low, high], axis=0))
            for e in range(2):
                lines[pl.ds(i * 8 + 2 * pair + e, KX, stride=PITCH), :] = modes[:, 128 * e : 128 * (e + 1)]

    def left_copy(p, x, modes, first, count):
        peer = left_peer(p, 1)
        return pltpu.make_async_remote_copy(
            src_ref=t1.at[pl.ds(KX // 2 + peer * XA + x, modes), pl.ds(pl.multiple_of(first, 8), count), :],
            dst_ref=r1.at[pl.ds(x, modes), left, pl.ds(pl.multiple_of(first, 8), count), :],
            send_sem=lsend.at[x],
            recv_sem=lrecv.at[x],
            device_id=(peer, right),
            device_id_type=MESH,
        )

    def w_copy(b, half, d):
        peer = right_peer(d, 1)
        return pltpu.make_async_remote_copy(
            src_ref=t1.at[pl.ds(peer * LEFT + half * 8, 8), pl.ds(pl.multiple_of(b * 16, 16), 16), :],
            dst_ref=w.at[pl.ds((b * RIGHT + right) * LEFT + half * 8, 8)],
            send_sem=wsend.at[b],
            recv_sem=wrecv.at[b],
            device_id=(left, peer),
            device_id_type=MESH,
        )

    def x_step(b, carry):
        slab_copy(2 * b).wait()

        @pl.when(b < 3)
        def _():
            slab_copy(2 * b + 2).start()
            slab_copy(2 * b + 3).start()

        @pl.when(b == 3)
        def _():
            for copy in table_copies[1:]:
                copy.start()

        x_slab(2 * b)
        slab_copy(2 * b + 1).wait()
        x_slab(2 * b + 1)

        @pl.when(b == 0)
        def _():
            pl.semaphore_wait(barrier, LEFT + RIGHT - 2)

        def send_w(j, carry):
            w_copy(b, j // (RIGHT - 1), j % (RIGHT - 1) + 1).start()
            return carry

        def send_left(j, carry):
            left_copy(j + 1, 0, EARLY, b * 16, 16).start()
            return carry

        lax.fori_loop(0, 2 * (RIGHT - 1), send_w, 0)
        lax.fori_loop(0, LEFT - 1, send_left, 0)
        return carry

    lax.fori_loop(0, 4, x_step, 0)

    def send_left(j, carry):
        left_copy(j % (LEFT - 1) + 1, EARLY + j // (LEFT - 1), 1, 0, 64).start()
        return carry

    def own_left(x, carry):
        r1[x, left] = t1[KX // 2 + left * XA + x, 0:64, :]
        return carry

    lax.fori_loop(0, XA, own_left, 0)

    def own_w(j, carry):
        for b in range(4):
            w[(b * RIGHT + right) * LEFT + j] = t1[right * LEFT + j, 16 * b : 16 * (b + 1), :]
        return carry

    lax.fori_loop(0, LEFT, own_w, 0)

    table_copies[1].wait()
    table_copies[2].wait()
    table_copies[3].wait()

    def z_rows(a, carry):
        cos_a, sin_a = coarse[0, pl.ds(a, 1), :], coarse[1, pl.ds(a, 1), :]
        block = cos_a * fine[0] - sin_a * fine[1]
        high, low = parts(block)
        for n in range(4):
            ztable[n, pl.ds(pl.multiple_of(a * FINE, FINE), FINE), :] = high[:, 256 * n : 256 * (n + 1)]
            ztable[n, pl.ds(pl.multiple_of(NZ + a * FINE, FINE), FINE), :] = low[:, 256 * n : 256 * (n + 1)]
        return carry

    lax.fori_loop(0, NZ // FINE, z_rows, 0)

    def right_copy(x, d):
        peer = right_peer(d, 1)
        return pltpu.make_async_remote_copy(
            src_ref=t2.at[x, pl.ds(pl.multiple_of(peer * YO, YO), YO), :],
            dst_ref=q.at[x, right],
            send_sem=qsend.at[x],
            recv_sem=qrecv.at[x],
            device_id=(left, peer),
            device_id_type=MESH,
        )

    def u_copy(k, p):
        peer = left_peer(p, 1)
        return pltpu.make_async_remote_copy(
            src_ref=v.at[k, pl.ds(pl.multiple_of(peer * 8, 8), 8), :],
            dst_ref=u.at[pl.ds(pl.multiple_of(left * YL + 8 * k, 8), 8), :],
            send_sem=usend,
            recv_sem=urecv,
            device_id=(peer, right),
            device_id_type=MESH,
        )

    def b_copy(n, d):
        peer = right_peer(d, 1)
        return pltpu.make_async_remote_copy(
            src_ref=t3.at[pl.ds(pl.multiple_of(peer * YO, YO), YO), pl.ds(256 * n, 256)],
            dst_ref=result.at[XA + right, :, pl.ds(256 * n, 256)],
            send_sem=bsend,
            recv_sem=brecv,
            device_id=(left, peer),
            device_id_type=MESH,
        )

    def out_copy(k):
        return pltpu.make_async_copy(result.at[pl.ds(2 * k, 2)], o_ref.at[pl.ds(2 * k, 2)], out_sem.at[k])

    def arrived(ref, sem):
        pltpu.make_async_copy(ref, ref, sem).wait()

    def left_bytes(x, modes):
        return r1.at[pl.ds(x, modes), pl.ds(0, LEFT - 1)]

    def right_bytes(x):
        return q.at[x, pl.ds(0, RIGHT - 1)]

    def w_bytes(b):
        return w.at[pl.ds(b * RIGHT * LEFT, (RIGHT - 1) * LEFT)]

    def u_bytes():
        return u.at[pl.ds(0, NY - YL), :]

    def b_bytes():
        return result.at[pl.ds(XA, RIGHT - 1)]

    def ratio(of_xy, n):
        symbol = jnp.concatenate([of_xy, of_xy], axis=1) + sz_ref[:, 256 * n : 256 * (n + 1)]
        return (1.0 - 0.2 * symbol) / (1.0 + 0.2 * symbol)

    def z_modes(m, n):
        both = dot(zlhs[0 : 2 * m, :], ztable[n, 0:NZ, :])
        return both[0:m] + (both[m:] + dot(zlhs[0:m, :], ztable[n, NZ : 2 * NZ, :]))

    def y_of_first(x):
        @pl.when(x == 0)
        def _():
            arrived(left_bytes(0, EARLY), lrecv.at[0])

        @pl.when(x >= EARLY)
        def _():
            arrived(left_bytes(x, 1), lrecv.at[x])

        lines = r1[x].reshape(64, 2, 8, 128)
        data = jnp.concatenate([lines[:, e].reshape(NY, 128) for e in range(2)], axis=1)
        high, low = parts(data)
        t2[x] = dot(ytable[...], jnp.concatenate([high, low, high], axis=0))
        for d in range(1, RIGHT):
            right_copy(x, d).start()
        q[x, right] = t2[x, pl.ds(pl.multiple_of(right * YO, YO), YO), :]

    def z_of_first(k):
        for e in range(2):
            x = 2 * k + e
            arrived(right_bytes(x), qrecv.at[x])
            for j in range(RIGHT):
                high, low = parts(q[x, j])
                zlhs[32 * e : 32 * (e + 1), 256 * j : 256 * (j + 1)] = high
                zlhs[64 + 32 * e : 64 + 32 * (e + 1), 256 * j : 256 * (j + 1)] = low
        of_y = sym[pl.ds(pl.multiple_of(right * YO, YO), YO), :]
        for n in range(4):
            modes = z_modes(64, n)
            for e in range(2):
                x = 2 * k + e
                result[x, :, 256 * n : 256 * (n + 1)] = modes[32 * e : 32 * (e + 1)] * ratio(
                    sx_ref[left * XO + x] + of_y, n
                )
        out_copy(k).start()

    def z_of_second(k):
        arrived(w_bytes(k), wrecv.at[k])
        for j in range(RIGHT):
            lines = w[pl.ds((k * RIGHT + j) * LEFT, LEFT)].reshape(LEFT, 2, 8, 128)
            for half in range(2):
                high, low = parts(lines[:, half].reshape(128, 128))
                column = 256 * j + 128 * half
                zlhs[0:128, column : column + 128] = high
                zlhs[128:256, column : column + 128] = low
        for n in range(4):
            v[k, :, 256 * n : 256 * (n + 1)] = z_modes(128, n)

        def send(p, carry):
            u_copy(k, p).start()
            return carry

        lax.fori_loop(1, LEFT, send, 0)
        u[pl.ds(pl.multiple_of(left * YL + 8 * k, 8), 8), :] = v[k, pl.ds(pl.multiple_of(left * 8, 8), 8), :]

    def y_of_second():
        arrived(u_bytes(), urecv)
        of_xy = sx_ref[left * XO + XA + right] + sym[...]
        for n in range(4):
            high, low = parts(u[:, 256 * n : 256 * (n + 1)])
            modes = dot(ytable[...], jnp.concatenate([high, low, high], axis=0))
            t3[:, 256 * n : 256 * (n + 1)] = modes * ratio(of_xy, n)
            for d in range(1, RIGHT):
                b_copy(n, d).start()
        result[XA + right] = t3[pl.ds(pl.multiple_of(right * YO, YO), YO), :]

    def step(i, carry):
        @pl.when(i < 4)
        def _():
            z_of_second(i)
            sends = jnp.where(i < 3, i + 1, XA - EARLY) * (LEFT - 1)
            lax.fori_loop(i * (LEFT - 1), sends, send_left, 0)

        @pl.when(i == 4)
        def _():
            y_of_second()

        @pl.when(i == 7)
        def _():
            arrived(b_bytes(), brecv)
            for k in range(XA // 2, XO // 2):
                out_copy(k).start()

        def first(x, carry):
            y_of_first(x)
            return carry

        lax.fori_loop(jnp.where(i == 0, 0, i + 1), jnp.minimum(i + 2, XA), first, 0)

        @pl.when(i >= 4)
        def _():
            z_of_first(i - 4)

        return carry

    lax.fori_loop(0, 8, step, 0)

    def sent_first(x, carry):
        @pl.when(x == 0)
        def _():
            arrived(left_bytes(0, EARLY), lsend.at[0])

        @pl.when(x >= EARLY)
        def _():
            arrived(left_bytes(x, 1), lsend.at[x])

        arrived(right_bytes(x), qsend.at[x])
        return carry

    def sent_second(p, carry):
        arrived(w_bytes(p), wsend.at[p])
        return carry

    lax.fori_loop(0, XA, sent_first, 0)
    lax.fori_loop(0, 4, sent_second, 0)
    arrived(u_bytes(), usend)
    arrived(b_bytes(), bsend)
    for k in range(XO // 2):
        out_copy(k).wait()


def body(signal, symbol_x, symbol_y, symbol_z):
    coarse, fine = factor_tables(NZ)
    xtable = split_table(NX, x_order())
    ytable = split_table(NY, np.arange(KY))
    dma = pltpu.SemaphoreType.DMA
    any_space = pl.BlockSpec(memory_space=pl.ANY)
    smem = pl.BlockSpec(memory_space=pltpu.SMEM)
    vmem = pl.BlockSpec(memory_space=pltpu.VMEM)
    return pl.pallas_call(
        kernel,
        out_shape=jax.ShapeDtypeStruct((XO, YO, KZ), F32),
        in_specs=[any_space, any_space, any_space, any_space, any_space, smem, vmem, vmem],
        out_specs=any_space,
        scratch_shapes=[
            pltpu.VMEM((8, NX, 8, 128), F32),
            pltpu.VMEM(xtable.shape, BF16),
            pltpu.VMEM(ytable.shape, BF16),
            pltpu.VMEM(coarse.shape, F32),
            pltpu.VMEM(fine.shape, F32),
            pltpu.VMEM((4, 2 * NZ, 256), BF16),
            pltpu.VMEM((KX, PITCH, 128), F32),
            pltpu.VMEM((XA, LEFT, 64, 128), F32),
            pltpu.VMEM((XA, KY, ZL), F32),
            pltpu.VMEM((XA, RIGHT, YO, ZL), F32),
            pltpu.VMEM((4 * RIGHT * LEFT, 16, 128), F32),
            pltpu.VMEM((4, 8 * LEFT, KZ), F32),
            pltpu.VMEM((NY, KZ), F32),
            pltpu.VMEM((KY, KZ), F32),
            pltpu.VMEM((256, NZ), BF16),
            pltpu.VMEM((KY, 128), F32),
            pltpu.VMEM((XO, YO, KZ), F32),
            dma((8,)),
            dma((4,)),
            dma((XA,)),
            dma((XA,)),
            dma((XA,)),
            dma((XA,)),
            dma((4,)),
            dma((4,)),
            dma(()),
            dma(()),
            dma(()),
            dma(()),
            dma((XO // 2,)),
        ],
        compiler_params=pltpu.CompilerParams(
            collective_id=0, has_side_effects=True, vmem_limit_bytes=67043328
        ),
    )(
        signal,
        jnp.asarray(xtable),
        jnp.asarray(ytable),
        jnp.asarray(coarse),
        jnp.asarray(fine),
        symbol_x,
        symbol_y.reshape(1, NY),
        symbol_z.reshape(1, NZ),
    )


def solution(mesh):
    in_specs = (P(None, "left", "right"), P(), P(), P())
    out_specs = P("left", "right", None)
    return jax.shard_map(body, mesh=mesh, in_specs=in_specs, out_specs=out_specs, check_vma=False)
```

time: 118 us -> 98.6 us (0.84)
  Pallas kernels: 114 us -> 95.3 us
    pallas_call x1, Pallas kernels: 114 us -> 95.3 us  [body(): pl.pallas_call(kernel, out_shape=jax.ShapeDtypeStruct((XO, YO, KZ), F32),...]
where the time goes in v2:
time: 98.6 us; the launch traced here: 98.4 us
  Pallas kernels  95.3 us (97%)
  local copies, waits for them, and re-layouts  3.16 us (3%)
    pallas_call x1, Pallas kernels, body(): pl.pallas_call(kernel, out_shape=jax.ShapeDtypeStruct((XO, YO, KZ), F32),...  95.3 us
    unnamed x1, local copies, waits for them, and re-layouts  3.16 us

profile of v2, /device:TPU:1, one launch (start us, length us, event | category | flops | bytes accessed | tf_op | source)
XLA Modules:
  0.0 98.4 jit_solution(6269829748307075706)
XLA Ops:
  0.0 95.3 %shard_map.82 = f32[16,32,1024]{2,1,0:T(8,128)} custom-call(f32[512,32,256]{2,1,0:T(8,128)} %s_ref.1, bf16[256,1536]{1,0:T(8,128)(2,1)} %constant.8.clone.hx_ref, bf16[256,1536]{1,0:T(8,128)(2,1)} %constant.9.clone.hy_ref, f32[2,32,1024]{2,1,0:T(8,128)} %constant.10.clone.coarse_ref, f32[2,64,1024]{2,1,0:T(8,128)} %constant.11.clone.fine_ref, f32[512]{0:T(512)} %sx_ref.1, ...), custom_call_target="tpu_custom_call" | custom-call | tf_op jit(solution)/shard_map/pallas_call | solution.py:401
  95.3 3.2 %copy.10 = f32[16,32,1024]{2,1,0:T(8,128)} copy(f32[16,32,1024]{2,1,0:T(8,128)} %shard_map.82) | data formatting | bytes 4194304

commit v3 on v2

--- a/solution.py
+++ b/solution.py
@@ -67,9 +67,9 @@
 
 
 def kernel(
-    s_ref, hx_ref, hy_ref, coarse_ref, fine_ref, sx_ref, sy_ref, sz_ref, o_ref,
-    slabs, xtable, ytable, coarse, fine, ztable, t1, r1, t2, q, w, v, u, t3, zlhs, sym, result,
-    slab_sem, table_sem, lsend, lrecv, qsend, qrecv, wsend, wrecv, usend, urecv, bsend, brecv, out_sem,
+    s_ref, hx_ref, hy_ref, coarse_ref, fine_ref, x_ref, y_ref, z_ref, result,
+    slabs, xtable, ytable, coarse, fine, ztable, t1, r1, t2, q, w, v, u, t3, zlhs, sym, sx, sy, sz,
+    slab_sem, table_sem, lsend, lrecv, qsend, qrecv, wsend, wrecv, usend, urecv, bsend, brecv,
 ):
     left = lax.axis_index("left")
     right = lax.axis_index("right")
@@ -99,13 +99,14 @@
         pltpu.make_async_copy(coarse_ref, coarse, table_sem.at[1]),
         pltpu.make_async_copy(fine_ref, fine, table_sem.at[2]),
         pltpu.make_async_copy(hy_ref, ytable, table_sem.at[3]),
+        pltpu.make_async_copy(x_ref, sx, table_sem.at[4]),
+        pltpu.make_async_copy(y_ref, sy, table_sem.at[5]),
+        pltpu.make_async_copy(z_ref, sz, table_sem.at[6]),
     ]
     slab_copy(0).start()
     table_copies[0].start()
     slab_copy(1).start()
     table_copies[0].wait()
-
-    sym[...] = jnp.broadcast_to(sy_ref[:, 0:KY], (128, KY)).T
 
     def x_slab(i):
         rows = slabs.at[i].reshape(NX * 8, 128)
@@ -130,13 +131,13 @@
             device_id_type=MESH,
         )
 
-    def w_copy(b, half, d):
+    def w_copy(i, d):
         peer = right_peer(d, 1)
         return pltpu.make_async_remote_copy(
-            src_ref=t1.at[pl.ds(peer * LEFT + half * 8, 8), pl.ds(pl.multiple_of(b * 16, 16), 16), :],
-            dst_ref=w.at[pl.ds((b * RIGHT + right) * LEFT + half * 8, 8)],
-            send_sem=wsend.at[b],
-            recv_sem=wrecv.at[b],
+            src_ref=t1.at[pl.ds(peer * LEFT, LEFT), pl.ds(pl.multiple_of(i * 8, 8), 8), :],
+            dst_ref=w.at[pl.ds((i // 2 * RIGHT + right) * LEFT, LEFT), pl.ds(pl.multiple_of(i % 2 * 8, 8), 8), :],
+            send_sem=wsend.at[i // 2],
+            recv_sem=wrecv.at[i // 2],
             device_id=(left, peer),
             device_id_type=MESH,
         )
@@ -155,22 +156,22 @@
                 copy.start()
 
         x_slab(2 * b)
+
+        @pl.when(b == 0)
+        def _():
+            pl.semaphore_wait(barrier, LEFT + RIGHT - 2)
+
+        for d in range(1, RIGHT):
+            w_copy(2 * b, d).start()
         slab_copy(2 * b + 1).wait()
         x_slab(2 * b + 1)
-
-        @pl.when(b == 0)
-        def _():
-            pl.semaphore_wait(barrier, LEFT + RIGHT - 2)
-
-        def send_w(j, carry):
-            w_copy(b, j // (RIGHT - 1), j % (RIGHT - 1) + 1).start()
-            return carry
+        for d in range(1, RIGHT):
+            w_copy(2 * b + 1, d).start()
 
         def send_left(j, carry):
             left_copy(j + 1, 0, EARLY, b * 16, 16).start()
             return carry
 
-        lax.fori_loop(0, 2 * (RIGHT - 1), send_w, 0)
         lax.fori_loop(0, LEFT - 1, send_left, 0)
         return carry
 
@@ -179,6 +180,8 @@
     def send_left(j, carry):
         left_copy(j % (LEFT - 1) + 1, EARLY + j // (LEFT - 1), 1, 0, 64).start()
         return carry
+
+    lax.fori_loop(0, LEFT - 1, send_left, 0)
 
     def own_left(x, carry):
         r1[x, left] = t1[KX // 2 + left * XA + x, 0:64, :]
@@ -193,9 +196,9 @@
 
     lax.fori_loop(0, LEFT, own_w, 0)
 
-    table_copies[1].wait()
-    table_copies[2].wait()
-    table_copies[3].wait()
+    for copy in table_copies[1:]:
+        copy.wait()
+    sym[...] = jnp.broadcast_to(sy[:, 0:KY], (128, KY)).T
 
     def z_rows(a, carry):
         cos_a, sin_a = coarse[0, pl.ds(a, 1), :], coarse[1, pl.ds(a, 1), :]
@@ -233,17 +236,14 @@
     def b_copy(n, d):
         peer = right_peer(d, 1)
         return pltpu.make_async_remote_copy(
-            src_ref=t3.at[pl.ds(pl.multiple_of(peer * YO, YO), YO), pl.ds(256 * n, 256)],
-            dst_ref=result.at[XA + right, :, pl.ds(256 * n, 256)],
+            src_ref=t3.at[pl.ds(pl.multiple_of(peer * YO, YO), YO), pl.ds(pl.multiple_of(256 * n, 256), 256)],
+            dst_ref=result.at[XA + right, :, pl.ds(pl.multiple_of(256 * n, 256), 256)],
             send_sem=bsend,
             recv_sem=brecv,
             device_id=(left, peer),
             device_id_type=MESH,
         )
 
-    def out_copy(k):
-        return pltpu.make_async_copy(result.at[pl.ds(2 * k, 2)], o_ref.at[pl.ds(2 * k, 2)], out_sem.at[k])
-
     def arrived(ref, sem):
         pltpu.make_async_copy(ref, ref, sem).wait()
 
@@ -263,7 +263,7 @@
         return result.at[pl.ds(XA, RIGHT - 1)]
 
     def ratio(of_xy, n):
-        symbol = jnp.concatenate([of_xy, of_xy], axis=1) + sz_ref[:, 256 * n : 256 * (n + 1)]
+        symbol = jnp.concatenate([of_xy, of_xy], axis=1) + sz[:, 256 * n : 256 * (n + 1)]
         return (1.0 - 0.2 * symbol) / (1.0 + 0.2 * symbol)
 
     def z_modes(m, n):
@@ -301,9 +301,8 @@
             for e in range(2):
                 x = 2 * k + e
                 result[x, :, 256 * n : 256 * (n + 1)] = modes[32 * e : 32 * (e + 1)] * ratio(
-                    sx_ref[left * XO + x] + of_y, n
+                    sx[left * XO + x] + of_y, n
                 )
-        out_copy(k).start()
 
     def z_of_second(k):
         arrived(w_bytes(k), wrecv.at[k])
@@ -326,45 +325,47 @@
 
     def y_of_second():
         arrived(u_bytes(), urecv)
-        of_xy = sx_ref[left * XO + XA + right] + sym[...]
+        of_xy = sx[left * XO + XA + right] + sym[...]
         for n in range(4):
             high, low = parts(u[:, 256 * n : 256 * (n + 1)])
             modes = dot(ytable[...], jnp.concatenate([high, low, high], axis=0))
             t3[:, 256 * n : 256 * (n + 1)] = modes * ratio(of_xy, n)
-            for d in range(1, RIGHT):
-                b_copy(n, d).start()
+            if n < 2:
+                for d in range(1, RIGHT):
+                    b_copy(n, d).start()
         result[XA + right] = t3[pl.ds(pl.multiple_of(right * YO, YO), YO), :]
 
     def step(i, carry):
         @pl.when(i < 4)
         def _():
             z_of_second(i)
-            sends = jnp.where(i < 3, i + 1, XA - EARLY) * (LEFT - 1)
-            lax.fori_loop(i * (LEFT - 1), sends, send_left, 0)
+            first = i + 1
+            last = jnp.where(i < 3, i + 2, XA - EARLY)
+            lax.fori_loop(first * (LEFT - 1), last * (LEFT - 1), send_left, 0)
 
         @pl.when(i == 4)
         def _():
             y_of_second()
 
-        @pl.when(i == 7)
-        def _():
-            arrived(b_bytes(), brecv)
-            for k in range(XA // 2, XO // 2):
-                out_copy(k).start()
+        @pl.when(i >= 4)
+        def _():
+            z_of_first(i - 4)
 
         def first(x, carry):
             y_of_first(x)
             return carry
 
-        lax.fori_loop(jnp.where(i == 0, 0, i + 1), jnp.minimum(i + 2, XA), first, 0)
-
-        @pl.when(i >= 4)
-        def _():
-            z_of_first(i - 4)
+        lax.fori_loop(jnp.where(i < 2, 2 * i, jnp.minimum(i + 2, XA)), jnp.where(i < 1, 2, jnp.minimum(i + 3, XA)), first, 0)
+
+        @pl.when((i == 4) | (i == 5))
+        def _():
+            for d in range(1, RIGHT):
+                b_copy(i - 2, d).start()
 
         return carry
 
     lax.fori_loop(0, 8, step, 0)
+    arrived(b_bytes(), brecv)
 
     def sent_first(x, carry):
         @pl.when(x == 0)
@@ -386,8 +387,6 @@
     lax.fori_loop(0, 4, sent_second, 0)
     arrived(u_bytes(), usend)
     arrived(b_bytes(), bsend)
-    for k in range(XO // 2):
-        out_copy(k).wait()
 
 
 def body(signal, symbol_x, symbol_y, symbol_z):
@@ -396,13 +395,12 @@
     ytable = split_table(NY, np.arange(KY))
     dma = pltpu.SemaphoreType.DMA
     any_space = pl.BlockSpec(memory_space=pl.ANY)
-    smem = pl.BlockSpec(memory_space=pltpu.SMEM)
     vmem = pl.BlockSpec(memory_space=pltpu.VMEM)
     return pl.pallas_call(
         kernel,
-        out_shape=jax.ShapeDtypeStruct((XO, YO, KZ), F32),
-        in_specs=[any_space, any_space, any_space, any_space, any_space, smem, vmem, vmem],
-        out_specs=any_space,
+        out_shape=pltpu.VMEM((XO, YO, KZ), F32),
+        in_specs=[any_space] * 8,
+        out_specs=vmem,
         scratch_shapes=[
             pltpu.VMEM((8, NX, 8, 128), F32),
             pltpu.VMEM(xtable.shape, BF16),
@@ -420,9 +418,11 @@
             pltpu.VMEM((KY, KZ), F32),
             pltpu.VMEM((256, NZ), BF16),
             pltpu.VMEM((KY, 128), F32),
-            pltpu.VMEM((XO, YO, KZ), F32),
+            pltpu.SMEM((NX,), F32),
+            pltpu.VMEM((1, NY), F32),
+            pltpu.VMEM((1, NZ), F32),
             dma((8,)),
-            dma((4,)),
+            dma((7,)),
             dma((XA,)),
             dma((XA,)),
             dma((XA,)),
@@ -433,10 +433,9 @@
             dma(()),
             dma(()),
             dma(()),
-            dma((XO // 2,)),
         ],
         compiler_params=pltpu.CompilerParams(
-            collective_id=0, has_side_effects=True, vmem_limit_bytes=67043328
+            collective_id=0, has_side_effects=True, vmem_limit_bytes=58 * 2**20
         ),
     )(
         signal,

time: 98.6 us -> 91.6 us (0.929)
  Pallas kernels: 95.3 us -> 90.1 us
  local copies, waits for them, and re-layouts: 3.16 us -> 1.32 us
    pallas_call x1, Pallas kernels: 95.3 us -> 90.1 us  [body(): pl.pallas_call(kernel, out_shape=pltpu.VMEM((XO, YO, KZ), F32), in_specs=...]
    unnamed x1, local copies, waits for them, and re-layouts: 3.16 us -> 1.32 us
where the time goes in v3:
time: 91.6 us; the launch traced here: 91.5 us
  Pallas kernels  90.1 us (98%)
  local copies, waits for them, and re-layouts  1.32 us (1%)
    pallas_call x1, Pallas kernels, body(): pl.pallas_call(kernel, out_shape=pltpu.VMEM((XO, YO, KZ), F32), in_specs=...  90.1 us

profile of v3, /device:TPU:1, one launch (start us, length us, event | category | flops | bytes accessed | tf_op | source)
XLA Modules:
  0.0 91.5 jit_solution(9023503832132468926)
XLA Ops:
  0.0 90.1 %shard_map.82 = f32[16,32,1024]{2,1,0:T(8,128)S(1)} custom-call(f32[512,32,256]{2,1,0:T(8,128)} %s_ref.1, bf16[256,1536]{1,0:T(8,128)(2,1)} %constant.8.clone.hx_ref, bf16[256,1536]{1,0:T(8,128)(2,1)} %constant.9.clone.hy_ref, f32[2,32,1024]{2,1,0:T(8,128)} %constant.10.clone.coarse_ref, f32[2,64,1024]{2,1,0:T(8,128)} %constant.11.clone.fine_ref, f32[512]{0:T(512)} %x_ref.1, ...), custom_call_target="tpu_custom_call" | custom-call | tf_op jit(solution)/shard_map/pallas_call | solution.py:399
  90.1 1.3 %copy.10 = f32[16,32,1024]{2,1,0:T(8,128)} copy(f32[16,32,1024]{2,1,0:T(8,128)S(1)} %shard_map.82) | data formatting | bytes 4194304

commit v4 on v3

--- a/solution.py
+++ b/solution.py
@@ -69,7 +69,7 @@
 def kernel(
     s_ref, hx_ref, hy_ref, coarse_ref, fine_ref, x_ref, y_ref, z_ref, result,
     slabs, xtable, ytable, coarse, fine, ztable, t1, r1, t2, q, w, v, u, t3, zlhs, sym, sx, sy, sz,
-    slab_sem, table_sem, lsend, lrecv, qsend, qrecv, wsend, wrecv, usend, urecv, bsend, brecv,
+    ready, slab_sem, table_sem, lsend, lrecv, qsend, qrecv, wsend, wrecv, usend, urecv, bsend, brecv,
 ):
     left = lax.axis_index("left")
     right = lax.axis_index("right")
@@ -81,11 +81,15 @@
     def right_peer(p, sign):
         return ((right // 2 + sign * (p // 2) + 4) % 4) * 2 + (right + p) % 2
 
+    def plane_peer(d, along):
+        return left_peer(4 * d if along == 0 else d, 1)
+
     barrier = pltpu.get_barrier_semaphore()
-    for p in range(1, LEFT):
-        pl.semaphore_signal(barrier, inc=1, device_id=(left_peer(p, -1), right), device_id_type=MESH)
-    for p in range(1, RIGHT):
-        pl.semaphore_signal(barrier, inc=1, device_id=(left, right_peer(p, -1)), device_id_type=MESH)
+    for d in range(1, RIGHT):
+        pl.semaphore_signal(barrier, inc=1, device_id=(left, right_peer(d, -1)), device_id_type=MESH)
+    for along in range(2):
+        for d in range(1, 4):
+            pl.semaphore_signal(barrier, inc=1, device_id=(plane_peer(d, along), right), device_id_type=MESH)
 
     def slab_copy(i):
         return pltpu.make_async_copy(
@@ -108,7 +112,7 @@
     slab_copy(1).start()
     table_copies[0].wait()
 
-    def x_slab(i):
+    def x_slab(i, first, last):
         rows = slabs.at[i].reshape(NX * 8, 128)
         lines = t1.reshape(KX * PITCH, 128)
         for pair in range(4):
@@ -116,9 +120,10 @@
                 [rows[pl.ds(2 * pair + e, NX, stride=8), :] for e in range(2)], axis=1
             )
             high, low = parts(data)
-            modes = dot(xtable[...], jnp.concatenate([high, low, high], axis=0))
+            modes = dot(xtable[first:last, :], jnp.concatenate([high, low, high], axis=0))
             for e in range(2):
-                lines[pl.ds(i * 8 + 2 * pair + e, KX, stride=PITCH), :] = modes[:, 128 * e : 128 * (e + 1)]
+                start = first * PITCH + i * 8 + 2 * pair + e
+                lines[pl.ds(start, last - first, stride=PITCH), :] = modes[:, 128 * e : 128 * (e + 1)]
 
     def left_copy(p, x, modes, first, count):
         peer = left_peer(p, 1)
@@ -142,6 +147,32 @@
             device_id_type=MESH,
         )
 
+    def send_w(i):
+        for d in range(1, RIGHT):
+            w_copy(i, d).start()
+
+    def send_early(b):
+        def send(j, carry):
+            left_copy(j + 1, 0, EARLY, b * 16, 16).start()
+            return carry
+
+        lax.fori_loop(0, LEFT - 1, send, 0)
+
+    slab_copy(0).wait()
+    slab_copy(2).start()
+    slab_copy(3).start()
+    x_slab(0, 0, KX // 2)
+    pl.semaphore_wait(barrier, RIGHT - 1 + 6)
+    for d in range(1, 4):
+        pl.semaphore_signal(ready, inc=1, device_id=(plane_peer(d, 1), right), device_id_type=MESH)
+    send_w(0)
+    x_slab(0, KX // 2, KX)
+    slab_copy(1).wait()
+    x_slab(1, 0, KX)
+    send_w(1)
+    pl.semaphore_wait(ready, 3)
+    send_early(0)
+
     def x_step(b, carry):
         slab_copy(2 * b).wait()
 
@@ -155,27 +186,15 @@
             for copy in table_copies[1:]:
                 copy.start()
 
-        x_slab(2 * b)
-
-        @pl.when(b == 0)
-        def _():
-            pl.semaphore_wait(barrier, LEFT + RIGHT - 2)
-
-        for d in range(1, RIGHT):
-            w_copy(2 * b, d).start()
+        x_slab(2 * b, 0, KX)
+        send_w(2 * b)
         slab_copy(2 * b + 1).wait()
-        x_slab(2 * b + 1)
-        for d in range(1, RIGHT):
-            w_copy(2 * b + 1, d).start()
-
-        def send_left(j, carry):
-            left_copy(j + 1, 0, EARLY, b * 16, 16).start()
-            return carry
-
-        lax.fori_loop(0, LEFT - 1, send_left, 0)
-        return carry
-
-    lax.fori_loop(0, 4, x_step, 0)
+        x_slab(2 * b + 1, 0, KX)
+        send_w(2 * b + 1)
+        send_early(b)
+        return carry
+
+    lax.fori_loop(1, 4, x_step, 0)
 
     def send_left(j, carry):
         left_copy(j % (LEFT - 1) + 1, EARLY + j // (LEFT - 1), 1, 0, 64).start()
@@ -365,8 +384,6 @@
         return carry
 
     lax.fori_loop(0, 8, step, 0)
-    arrived(b_bytes(), brecv)
-
     def sent_first(x, carry):
         @pl.when(x == 0)
         def _():
@@ -386,6 +403,7 @@
     lax.fori_loop(0, XA, sent_first, 0)
     lax.fori_loop(0, 4, sent_second, 0)
     arrived(u_bytes(), usend)
+    arrived(b_bytes(), brecv)
     arrived(b_bytes(), bsend)
 
 
@@ -421,6 +439,7 @@
             pltpu.SMEM((NX,), F32),
             pltpu.VMEM((1, NY), F32),
             pltpu.VMEM((1, NZ), F32),
+            pltpu.SemaphoreType.REGULAR,
             dma((8,)),
             dma((7,)),
             dma((XA,)),

time: 91.6 us -> 91.3 us (level)
  no operation moved by 1% of the time
where the time goes in v4:
time: 91.3 us; the launch traced here: 91.2 us
  Pallas kernels  89.8 us (98%)
  local copies, waits for them, and re-layouts  1.32 us (1%)
    pallas_call x1, Pallas kernels, body(): pl.pallas_call(kernel, out_shape=pltpu.VMEM((XO, YO, KZ), F32), in_specs=...  89.8 us

profile of v4, /device:TPU:1, one launch (start us, length us, event | category | flops | bytes accessed | tf_op | source)
XLA Modules:
  0.0 91.2 jit_solution(5856029569838572895)
XLA Ops:
  0.0 89.8 %shard_map.82 = f32[16,32,1024]{2,1,0:T(8,128)S(1)} custom-call(f32[512,32,256]{2,1,0:T(8,128)} %s_ref.1, bf16[256,1536]{1,0:T(8,128)(2,1)} %constant.8.clone.hx_ref, bf16[256,1536]{1,0:T(8,128)(2,1)} %constant.9.clone.hy_ref, f32[2,32,1024]{2,1,0:T(8,128)} %constant.10.clone.coarse_ref, f32[2,64,1024]{2,1,0:T(8,128)} %constant.11.clone.fine_ref, f32[512]{0:T(512)} %x_ref.1, ...), custom_call_target="tpu_custom_call" | custom-call | tf_op jit(solution)/shard_map/pallas_call | solution.py:417
  89.8 1.3 %copy.10 = f32[16,32,1024]{2,1,0:T(8,128)} copy(f32[16,32,1024]{2,1,0:T(8,128)S(1)} %shard_map.82) | data formatting | bytes 4194304
